TPU v7x, 32 devices: a whole 2x2x4 slice. The times are simulated.
32 devices in a mesh: dp: 8 (over z, y), tensor: 4 (over x, core).
Axes of the slice: x: 2, y: 2, z: 4, core: 2. Of those that a mesh axis runs over, the one named last changes fastest.
Arguments:
- acts: bfloat16 [8, 2048, 1024], P('dp', 'tensor'), may hold values from -6 to 6
- grad_out: bfloat16 [8, 2048, 1024], P('dp', 'tensor'), may hold values from -6 to 6
- norm_gain: float32 [1024], replicated, may hold values from 0.5 to 1.5
- w_zx: bfloat16 [1024, 2, 2048], P('dp', None, 'tensor'), may hold values from -0.1875 to 0.1875
- w_bc: bfloat16 [1024, 256], P('dp'), may hold values from -0.1875 to 0.1875
- w_dt: bfloat16 [1024, 32], P('dp', 'tensor'), may hold values from -0.1875 to 0.1875
- w_out: bfloat16 [1024, 2048], P('dp', 'tensor'), may hold values from -0.125 to 0.125
- conv_x: float32 [4, 2048], replicated, may hold values from -3 to 3
- conv_x_bias: float32 [2048], replicated, may hold values from -0.5 to 0.5
- conv_bc: float32 [4, 256], replicated, may hold values from -3 to 3
- conv_bc_bias: float32 [256], replicated, may hold values from -0.5 to 0.5
- dt_bias: float32 [32], replicated, may hold values from -7 to -2
- a_log: float32 [32], replicated, may hold values from 0 to 2.77
- d_skip: float32 [32], replicated, may hold values from 0.5 to 1.5
- gate_gain: float32 [2048], replicated, may hold values from 0.5 to 1.5
Outputs:
- out_acts: bfloat16 [8, 2048, 1024], P('dp', 'tensor')
- grad_acts: float32 [8, 2048, 1024], P('dp', 'tensor')
- grad_norm_gain: float32 [1024], replicated
- grad_w_zx: float32 [1024, 2, 2048], P('dp', None, 'tensor')
- grad_w_bc: float32 [1024, 256], P('dp')
- grad_w_dt: float32 [1024, 32], P('dp', 'tensor')
- grad_w_out: float32 [1024, 2048], P('dp', 'tensor')
- grad_conv_x: float32 [4, 2048], replicated
- grad_conv_x_bias: float32 [2048], replicated
- grad_conv_bc: float32 [4, 256], replicated
- grad_conv_bc_bias: float32 [256], replicated
- grad_dt_bias: float32 [32], replicated
- grad_a_log: float32 [32], replicated
- grad_d_skip: float32 [32], replicated
- grad_gate_gain: float32 [2048], replicated
All inputs are finite; a program needn't handle non-finite values.
Results may differ from a plain program's by a relative error of at most 0.0096.
Values may be sent and summed in bfloat16 or wider, within the bound.
A program may use at most 192 MiB of HBM per device.

v0:
```python
import jax
import jax.numpy as jnp
from jax import lax
from jax.sharding import PartitionSpec as P

BLOCK_LEN = 256


EPSILON = 1e-05
FULL_PRECISION = lax.Precision.HIGHEST
CONTRACT_LAST = (((1,), (1,)), ((), ()))
CONTRACT_FIRST = (((0,), (0,)), ((), ()))


def causal_conv(values, conv_taps):
    tap_count = conv_taps.shape[0]
    length = values.shape[0]
    padded = jnp.pad(values, ((tap_count - 1, 0), (0, 0)))
    result = conv_taps[0] * padded[0:length]
    for offset in range(1, tap_count):
        result = result + conv_taps[offset] * padded[offset : offset + length]
    return result


def ssd_scan(x_heads, step_dt, decay_rate, b_mat, c_mat, block_size):
    length, head_count, head_width = x_heads.shape
    state_count = b_mat.shape[1]
    block_count = length // block_size
    x_blocks = x_heads.reshape(block_count, block_size, head_count, head_width)
    dt_blocks = step_dt.reshape(block_count, block_size, head_count)
    b_blocks = b_mat.reshape(block_count, block_size, state_count)
    c_blocks = c_mat.reshape(block_count, block_size, state_count)
    positions = jnp.arange(block_size)
    causal_mask = (positions[:, None] >= positions[None, :]).astype(jnp.float32)

    def step_block(state, inputs):
        x_block, dt_block, b_block, c_block = inputs
        cum_logs = jnp.cumsum(dt_block * decay_rate[None, :], axis=0)
        scores = jnp.dot(c_block, b_block.T, precision=FULL_PRECISION)
        log_gaps = (cum_logs[:, None, :] - cum_logs[None, :, :]) * causal_mask[:, :, None]
        weights = (
            scores[:, :, None] * jnp.exp(log_gaps) * causal_mask[:, :, None] * dt_block[None, :, :]
        )
        within = jnp.einsum("ijh,jhp->ihp", weights, x_block, precision=FULL_PRECISION)
        carried = (
            jnp.einsum("in,hpn->ihp", c_block, state, precision=FULL_PRECISION)
            * jnp.exp(cum_logs)[:, :, None]
        )
        block_total = cum_logs[-1]
        state_weight = jnp.exp(block_total[None, :] - cum_logs) * dt_block
        update = jnp.einsum(
            "jhp,jn->hpn", x_block * state_weight[:, :, None], b_block, precision=FULL_PRECISION
        )
        new_state = state * jnp.exp(block_total)[:, None, None] + update
        return (new_state, within + carried)

    zero_state = jnp.zeros((head_count, head_width, state_count), jnp.float32)
    final_state, outputs = lax.scan(
        jax.checkpoint(step_block), zero_state, (x_blocks, dt_blocks, b_blocks, c_blocks)
    )
    return outputs.reshape(length, head_count, head_width)


def pre_norm(acts_row, norm_gain):
    return (
        acts_row
        * lax.rsqrt(jnp.mean(acts_row * acts_row, axis=-1, keepdims=True) + EPSILON)
        * norm_gain
    )


def conv_part(x_vals, bc_vals, x_taps, x_shift, bc_taps, bc_shift):
    x_conv = jax.nn.silu(causal_conv(x_vals, x_taps) + x_shift)
    bc_conv = jax.nn.silu(causal_conv(bc_vals, bc_taps) + bc_shift)
    return (x_conv, bc_conv)


def mix_part(x_vals, b_vals, c_vals, dt_vals, dt_shift, log_rate, skip_gain, gate_vals):
    length = x_vals.shape[0]
    head_count = dt_vals.shape[1]
    x_heads = x_vals.reshape(length, head_count, -1)
    step_dt = jax.nn.softplus(dt_vals + dt_shift)
    mixed = (
        ssd_scan(x_heads, step_dt, -jnp.exp(log_rate), b_vals, c_vals, BLOCK_LEN)
        + skip_gain[None, :, None] * x_heads
    )
    return mixed.reshape(length, -1) * jax.nn.silu(gate_vals)


def widen(piece, start, full_size):
    holder = jnp.zeros(piece.shape[:-1] + (full_size,), jnp.float32)
    return lax.dynamic_update_slice_in_dim(holder, piece, start, piece.ndim - 1)


def body(
    acts,
    grad_out,
    norm_gain,
    w_zx,
    w_bc,
    w_dt,
    w_out,
    conv_x,
    conv_x_bias,
    conv_bc,
    conv_bc_bias,
    dt_bias,
    a_log,
    d_skip,
    gate_gain,
):
    parts = lax.axis_size("tensor")
    rank = lax.axis_index("tensor")
    local_rows = acts.shape[1]
    channels = w_zx.shape[2]
    head_count = w_dt.shape[1]
    state_count = w_bc.shape[1] // 2
    total_channels = channels * parts
    total_heads = head_count * parts
    chan_start = rank * channels
    head_start = rank * head_count
    zx_full, bc_full, dt_full, out_full = (
        lax.all_gather(w_zx, "dp", axis=0, tiled=True),
        lax.all_gather(w_bc, "dp", axis=0, tiled=True),
        lax.all_gather(w_dt, "dp", axis=0, tiled=True),
        lax.all_gather(w_out, "dp", axis=0, tiled=True),
    )
    acts_row = acts[0].astype(jnp.float32)
    normed_in, pre_back = jax.vjp(pre_norm, acts_row, norm_gain)
    hidden = lax.all_gather(normed_in.astype(jnp.bfloat16), "tensor", axis=0, tiled=True)
    zx_proj = jnp.einsum("ld,dkc->lkc", hidden, zx_full, preferred_element_type=jnp.float32)
    bc_proj = jnp.dot(hidden, bc_full, preferred_element_type=jnp.float32)
    dt_proj = jnp.dot(hidden, dt_full, preferred_element_type=jnp.float32)
    conv_x_local = lax.dynamic_slice_in_dim(conv_x, chan_start, channels, 1)
    conv_xb_local = lax.dynamic_slice_in_dim(conv_x_bias, chan_start, channels, 0)
    dt_bias_local = lax.dynamic_slice_in_dim(dt_bias, head_start, head_count, 0)
    a_log_local = lax.dynamic_slice_in_dim(a_log, head_start, head_count, 0)
    d_skip_local = lax.dynamic_slice_in_dim(d_skip, head_start, head_count, 0)
    gain_local = lax.dynamic_slice_in_dim(gate_gain, chan_start, channels, 0)
    conv_outs, conv_back = jax.vjp(
        conv_part, zx_proj[:, 1], bc_proj, conv_x_local, conv_xb_local, conv_bc, conv_bc_bias
    )
    x_conv, bc_conv = conv_outs
    x_low = x_conv.astype(jnp.bfloat16)
    b_low = bc_conv[:, :state_count].astype(jnp.bfloat16)
    c_low = bc_conv[:, state_count:].astype(jnp.bfloat16)
    gated, mix_back = jax.vjp(
        mix_part,
        x_low.astype(jnp.float32),
        b_low.astype(jnp.float32),
        c_low.astype(jnp.float32),
        dt_proj,
        dt_bias_local,
        a_log_local,
        d_skip_local,
        zx_proj[:, 0],
    )
    square_total = lax.psum(jnp.sum(gated * gated, axis=1), "tensor")
    inv_rms = lax.rsqrt(square_total / total_channels + EPSILON)[:, None]
    mixed_out = (gated * inv_rms * gain_local).astype(jnp.bfloat16)
    projected = lax.psum_scatter(
        lax.dot_general(mixed_out, out_full, CONTRACT_LAST, preferred_element_type=jnp.float32),
        "tensor",
        scatter_dimension=0,
        tiled=True,
    )
    out_acts = (acts_row + projected).astype(jnp.bfloat16)[None]
    grad_row = grad_out[0]
    grad_rows_all = lax.all_gather(grad_row, "tensor", axis=0, tiled=True)
    grad_mixed = jnp.dot(grad_rows_all, out_full, preferred_element_type=jnp.float32).astype(
        jnp.bfloat16
    )
    grad_out_w = lax.dot_general(
        grad_rows_all, mixed_out, CONTRACT_FIRST, preferred_element_type=jnp.float32
    )
    grad_normed = grad_mixed.astype(jnp.float32)
    grad_gain_local = jnp.sum(grad_normed * gated * inv_rms, axis=0)
    scaled = grad_normed * gain_local
    row_dot = lax.psum(jnp.sum(scaled * gated, axis=1), "tensor")
    grad_gated = (
        inv_rms * scaled
        - gated * (inv_rms * inv_rms * inv_rms) * (row_dot / total_channels)[:, None]
    )
    (
        grad_x_low,
        grad_b,
        grad_c,
        grad_dt_in,
        grad_dt_shift,
        grad_log_rate,
        grad_skip,
        grad_gate_in,
    ) = mix_back(grad_gated)
    grad_x_in, grad_bc_part, grad_x_taps, grad_x_shift, grad_bc_taps, grad_bc_shift = conv_back(
        (grad_x_low, jnp.concatenate([grad_b, grad_c], axis=1))
    )
    grad_bc_in = lax.psum(grad_bc_part, "tensor").astype(jnp.bfloat16)
    grad_zx = jnp.stack([grad_gate_in.astype(jnp.bfloat16), grad_x_in.astype(jnp.bfloat16)], axis=1)
    grad_dt_low = grad_dt_in.astype(jnp.bfloat16)
    grad_zx_w = jnp.einsum("ld,lkc->dkc", hidden, grad_zx, preferred_element_type=jnp.float32)
    grad_bc_w = lax.dot_general(
        hidden, grad_bc_in, CONTRACT_FIRST, preferred_element_type=jnp.float32
    )
    grad_dt_w = lax.dot_general(
        hidden, grad_dt_low, CONTRACT_FIRST, preferred_element_type=jnp.float32
    )
    from_zx = jnp.einsum("lkc,dkc->ld", grad_zx, zx_full, preferred_element_type=jnp.float32)
    grad_hidden = lax.psum_scatter(
        from_zx
        + lax.dot_general(grad_dt_low, dt_full, CONTRACT_LAST, preferred_element_type=jnp.float32),
        "tensor",
        scatter_dimension=0,
        tiled=True,
    )
    bc_piece = lax.dynamic_slice_in_dim(grad_bc_in, rank * local_rows, local_rows, 0)
    grad_hidden = grad_hidden + lax.dot_general(
        bc_piece, bc_full, CONTRACT_LAST, preferred_element_type=jnp.float32
    )
    grad_acts_norm, grad_norm_gain = pre_back(grad_hidden)
    grad_acts = (grad_row.astype(jnp.float32) + grad_acts_norm)[None]
    grad_w_zx, grad_w_bc, grad_w_dt, grad_w_out = (
        lax.psum_scatter(grad_zx_w, "dp", scatter_dimension=0, tiled=True),
        lax.psum_scatter(grad_bc_w, "dp", scatter_dimension=0, tiled=True),
        lax.psum_scatter(grad_dt_w, "dp", scatter_dimension=0, tiled=True),
        lax.psum_scatter(grad_out_w, "dp", scatter_dimension=0, tiled=True),
    )
    small_sums = lax.psum(
        (
            grad_norm_gain,
            widen(grad_x_taps, chan_start, total_channels),
            widen(grad_x_shift, chan_start, total_channels),
            grad_bc_taps,
            grad_bc_shift,
            widen(grad_dt_shift, head_start, total_heads),
            widen(grad_log_rate, head_start, total_heads),
            widen(grad_skip, head_start, total_heads),
            widen(grad_gain_local, chan_start, total_channels),
        ),
        ("dp", "tensor"),
    )
    grad_ng, grad_cx, grad_cxb, grad_cbc, grad_cbcb, grad_dtb, grad_alog, grad_dsk, grad_gg = (
        small_sums
    )
    return (
        out_acts,
        grad_acts,
        grad_ng,
        grad_w_zx,
        grad_w_bc,
        grad_w_dt,
        grad_w_out,
        grad_cx,
        grad_cxb,
        grad_cbc,
        grad_cbcb,
        grad_dtb,
        grad_alog,
        grad_dsk,
        grad_gg,
    )


def solution(mesh):
    in_specs = (
        P("dp", "tensor", None),
        P("dp", "tensor", None),
        P(),
        P("dp", None, "tensor"),
        P("dp", None),
        P("dp", "tensor"),
        P("dp", "tensor"),
        P(),
        P(),
        P(),
        P(),
        P(),
        P(),
        P(),
        P(),
    )
    out_specs = (
        P("dp", "tensor", None),
        P("dp", "tensor", None),
        P(),
        P("dp", None, "tensor"),
        P("dp", None),
        P("dp", "tensor"),
        P("dp", "tensor"),
        P(),
        P(),
        P(),
        P(),
        P(),
        P(),
        P(),
        P(),
    )
    return jax.shard_map(body, mesh=mesh, in_specs=in_specs, out_specs=out_specs, check_vma=False)
```

profile of v0, /device:TPU:0, one launch (start us, length us, event | category | flops | bytes accessed | tf_op | source)
XLA Modules:
  0.0 917.9 jit_solution(7278153467009917441)
XLA Ops:
  16.2 27.8 %all_gather.19 = bf16[1024,8]{0,1:T(8,128)(2,1)S(1)} all-gather(bf16[128,8]{0,1:T(8,128)(2,1)S(1)} %copy-done.49), channel_id=1, replica_groups=mesh['dp'=8,'tensor'=4] {'dp'}, dimensions={0}, use_global_device_ids=true | all-gather | bytes 18432 | tf_op jit(solution)/shard_map/all_gather | solution.py:125
  44.0 32.3 %all_gather.21 = bf16[1024,256]{1,0:T(8,128)(2,1)S(1)} all-gather(bf16[128,256]{1,0:T(8,128)(2,1)S(1)} %copy-done.20), channel_id=1, replica_groups=mesh['dp'=8,'tensor'=4] {'dp'}, dimensions={0}, use_global_device_ids=true | all-gather | bytes 589824 | tf_op jit(solution)/shard_map/all_gather | solution.py:124
  86.0 15.5 %all-gather.8.cloned.1.call-done = bf16[1024,2,512]{2,0,1:T(8,128)(2,1)} async-done(((bf16[128,2,512]{2,0,1:T(8,128)(2,1)}), bf16[1024,2,512]{2,0,1:T(8,128)(2,1)}) %all-gather.8.cloned.1.call-update) | async-done | bytes 2097168 | tf_op jit(solution)/shard_map/all_gather | solution.py:123
  117.0 7.1 reshape.372
  137.5 87.5 %while.43 = (s32[]{:T(128)}, f32[8,64,128]{2,1,0:T(8,128)S(1)}, f32[8,256,8,64]{1,3,2,0:T(8,128)}, f32[8,8,64,128]{3,2,1,0:T(8,128)}, f32[8,256,8]{1,2,0:T(8,128...) while((s32[]{:T(128)}, f32[8,64,128]{2,1,0:T(8,128)S(1)}, ...), condition=%wide.region_4.5_spmd.clone.clone, body=%wide.region_1.4_spmd.clone.clone.sunk | while | flops 909711360 | bytes 5641051 | solution.py:58
  231.9 7.5 reshape.369
  239.4 7.6 multiply_reduce_fusion.8
  252.9 7.2 fusion.130
  260.2 7.4 fusion.96
  274.3 11.7 %multiply_reduce_fusion.3 = (f32[512]{0:T(512)}, f32[2048,512]{1,0:T(8,128)}, bf16[2048,1,512]{2,0,1:T(8,128)(2,1)}) fusion(f32[2048,512]{1,0:T(8,128)} %get-tuple-element.766, f32[2048,2,512]{2,0,1:T(8,128)} %copy-done.1, f32[2048]{0:T(1024)S(1)} %broadcast_multiply_fusion.8, f32[2048,512]{1,0:T(8,128)} %get-tuple-element.762, ...), kind=kLoop, calls=%fused_computation.161 | loop fusion | flops 30408192 | bytes 25196544 | tf_op jit(solution)/shard_map/transpose(jvp())/reduce_sum | solution.py:85
  286.0 7.1 reshape.370
  305.2 198.0 %while.42 = (s32[]{:T(128)}, f32[8]{0:T(128)}, f32[8,64,128]{2,1,0:T(8,128)S(1)}, f32[8,256,8,64]{1,3,2,0:T(8,128)}, f32[8,256,8]{1,2,0:T(8,128)}, /*index=5*/f3...) while((s32[]{:T(128)}, f32[8]{0:T(128)}, ...), condition=%wide.region_24.25_spmd.clone, body=%wide.region_10.0_spmd.clone.sunk | while | flops 2126610432 | bytes 15952340 | solution.py:58
  510.1 7.5 reshape.371
  517.6 11.5 %multiply_reduce_fusion.6 = (f32[512]{0:T(512)S(1)}, f32[512]{0:T(512)S(1)}, f32[512]{0:T(512)S(1)}, f32[512]{0:T(512)S(1)}, f32[512]{0:T(512)S(1)}, /*index=5*/f32[2048,512]{1,0:T(8,128)S(1)}) fusion(f32[2048,512]{1,0:T(8,128)} %copy-done, f32[2048,2,512]{2,0,1:T(8,128)} %copy-done.1, f32[2048,512]{1,0:T(8,128)} %get-tuple-element.766, ...), kind=kLoop, calls=%fused_computation.164 | loop fusion | flops 20968960 | bytes 25178112 | tf_op jit(solution)/shard_map/transpose(jvp())/reduce_sum | solution.py:21
  535.0 7.1 fusion.127
  542.2 8.2 fusion.107
  562.4 7.8 fusion.148
  579.6 40.8 %all-reduce.21 = bf16[2048,256]{1,0:T(8,128)(2,1)S(1)} all-reduce(f32[2048,256]{1,0:T(8,128)S(1)} %pad_add_fusion.3), channel_id=1, replica_groups=mesh['dp'=8,'tensor'=4] {'tensor'}, use_global_device_ids=true, to_apply=%region_26.27 | all-reduce | flops 524288 | bytes 3145728 | tf_op jit(solution)/shard_map/psum | solution.py:197
  628.8 8.3 reduce-scatter.11.cloned.1.call-done
  639.3 72.0 %reduce-scatter.9.cloned.1.call-done = f32[512,1024]{1,0:T(8,128)} async-done(((f32[2048,1024]{1,0:T(8,128)}), f32[512,1024]{1,0:T(8,128)}) %reduce-scatter.9.cloned.1.call-update) | async-done | bytes 2097168 | tf_op jit(solution)/shard_map/reduce_scatter | solution.py:208
  714.0 40.9 %all-reduce.19 = (f32[1024]{0:T(1024)}, f32[4,2048]{1,0:T(4,128)}, f32[2048]{0:T(1024)}, f32[4,256]{1,0:T(4,128)}, f32[256]{0:T(256)}, /*index=5*/f32[32]{0:T(128)}, f32[32]{0:T(128)}, f32[32]{0:T(128)}, f32[2048]{0:T(1024)}) all-reduce(f32[1024]{0:T(1024)S(1)} %get-tuple-element.689, ...), channel_id=1, replica_groups=mesh['dp'=8,'tensor'=4] {'dp','tensor'}, use_global_device_ids=true, to_apply=%region_29.30 | all-reduce | flops 14688 | bytes 117504 | tf_op jit(solution)/shard_map/psum | solution.py:227
  754.9 31.4 %reduce-scatter.7.cloned.1.call-done = f32[512,1024]{1,0:T(8,128)} async-done(((f32[2048,1024]{1,0:T(8,128)}), f32[512,1024]{1,0:T(8,128)}) %reduce-scatter.7.cloned.1.call-update) | async-done | bytes 2097168 | tf_op jit(solution)/shard_map/reduce_scatter | solution.py:161
  790.6 53.3 %reduce-scatter.15.cloned.1.call-done = f32[128,8]{0,1:T(8,128)} async-done(((f32[1024,8]{0,1:T(8,128)}), f32[128,8]{0,1:T(8,128)}) %reduce-scatter.15.cloned.1.call-update) | async-done | bytes 4112 | tf_op jit(solution)/shard_map/reduce_scatter | solution.py:224
  843.9 66.8 %reduce-scatter.13.cloned.1.call-done = f32[128,256]{1,0:T(8,128)} async-done(((f32[1024,256]{1,0:T(8,128)}), f32[128,256]{1,0:T(8,128)}) %reduce-scatter.13.cloned.1.call-update) | async-done | bytes 131088 | tf_op jit(solution)/shard_map/reduce_scatter | solution.py:223
  (623 shorter events, 414.4 us)
Async XLA Ops:
  7.2 36.8 %copy-start.20 = (bf16[128,256]{1,0:T(8,128)(2,1)S(1)}, bf16[128,256]{1,0:T(8,128)(2,1)}, u32[]{:S(2)}) copy-start(bf16[128,256]{1,0:T(8,128)(2,1)} %param.23) | copy-start | bytes 196612
  7.3 70.1 %all-gather.6.cloned.1.call-start = ((), (), s32[]{:S(2)}) async-start(), calls=%async_computation.6 | async-start | bytes 5242880 | tf_op jit(solution)/shard_map/all_gather | solution.py:130
  11.4 90.1 %all-gather.8.cloned.1.call-start = ((), (), s32[]{:S(2)}) async-start(), calls=%async_computation.7 | async-start | bytes 2359296 | tf_op jit(solution)/shard_map/all_gather | solution.py:123
  12.2 240.6 %all-gather.12.cloned.1.call-start = ((), (), s32[]{:S(2)}) async-start(), calls=%async_computation.15 | async-start | bytes 5242880 | tf_op jit(solution)/shard_map/all_gather | solution.py:169
  13.0 247.2 %all-gather.10.cloned.1.call-start = ((), (), s32[]{:S(2)}) async-start(), calls=%async_computation.8 | async-start | bytes 1179648 | tf_op jit(solution)/shard_map/all_gather | solution.py:126
  13.6 613.4 %reduce-scatter.17.cloned.1.call-start = ((), (), s32[]{:S(2)}) async-start(), calls=%async_computation.14 | async-start | bytes 2359296 | tf_op jit(solution)/shard_map/reduce_scatter | solution.py:225
  15.2 259.1 %copy-start.26 = (f32[512]{0:T(512)}, f32[512]{0:T(512)S(1)}, u32[]{:S(2)}) copy-start(f32[512]{0:T(512)S(1)} %dynamic_slice.100) | copy-start | bytes 6148
  16.1 258.2 %copy-start.22 = (f32[512]{0:T(512)}, f32[512]{0:T(512)S(1)}, u32[]{:S(2)}) copy-start(f32[512]{0:T(512)S(1)} %mul.863) | copy-start | bytes 6148
  16.2 65.0 %copy-start.39 = (f32[1,256]{1,0:T(1,128)}, f32[1,256]{1,0:T(1,128)S(1)}, u32[]{:S(2)}) copy-start(f32[1,256]{1,0:T(1,128)S(1)} %get-tuple-element.793) | copy-start | bytes 3076
  16.2 65.0 %copy-start.41 = (f32[1,256]{1,0:T(1,128)}, f32[1,256]{1,0:T(1,128)S(1)}, u32[]{:S(2)}) copy-start(f32[1,256]{1,0:T(1,128)S(1)} %get-tuple-element.794) | copy-start | bytes 3076
  16.2 65.0 %copy-start.43 = (f32[1,256]{1,0:T(1,128)}, f32[1,256]{1,0:T(1,128)S(1)}, u32[]{:S(2)}) copy-start(f32[1,256]{1,0:T(1,128)S(1)} %get-tuple-element.795) | copy-start | bytes 3076
  16.2 65.0 %copy-start.45 = (f32[1,256]{1,0:T(1,128)}, f32[1,256]{1,0:T(1,128)S(1)}, u32[]{:S(2)}) copy-start(f32[1,256]{1,0:T(1,128)S(1)} %get-tuple-element.796) | copy-start | bytes 3076
  44.0 87.0 %copy-start.18 = (bf16[1024,8]{0,1:T(8,128)(2,1)}, bf16[1024,8]{0,1:T(8,128)(2,1)S(1)}, u32[]{:S(2)}) copy-start(bf16[1024,8]{0,1:T(8,128)(2,1)S(1)} %all_gather.19) | copy-start | bytes 49156
  44.0 37.2 %copy-start.51 = (f32[256]{0:T(256)S(1)}, f32[256]{0:T(256)}, u32[]{:S(2)}) copy-start(f32[256]{0:T(256)} %param.29) | copy-start | bytes 3076
  77.3 35.0 %copy-start.28 = (f32[1,512]{1,0:T(1,128)}, f32[1,512]{1,0:T(1,128)S(1)}, u32[]{:S(2)}) copy-start(f32[1,512]{1,0:T(1,128)S(1)} %get-tuple-element.787) | copy-start | bytes 6148
  260.1 376.9 %reduce-scatter.11.cloned.1.call-start = ((), (), s32[]{:S(2)}) async-start(), calls=%async_computation.11 | async-start | bytes 4718592 | tf_op jit(solution)/shard_map/reduce_scatter | solution.py:222
  550.4 160.9 %reduce-scatter.9.cloned.1.call-start = ((), (), s32[]{:S(2)}) async-start(), calls=%async_computation.10 | async-start | bytes 10485760 | tf_op jit(solution)/shard_map/reduce_scatter | solution.py:208
  561.2 225.1 %reduce-scatter.7.cloned.1.call-start = ((), (), s32[]{:S(2)}) async-start(), calls=%async_computation.9 | async-start | bytes 10485760 | tf_op jit(solution)/shard_map/reduce_scatter | solution.py:161
  570.2 273.6 %reduce-scatter.15.cloned.1.call-start = ((), (), s32[]{:S(2)}) async-start(), calls=%async_computation.13 | async-start | bytes 36864 | tf_op jit(solution)/shard_map/reduce_scatter | solution.py:224
  620.5 90.8 %copy-start.4 = (bf16[1,512,1024]{2,1,0:T(8,128)(2,1)S(1)}, bf16[1,512,1024]{2,1,0:T(8,128)(2,1)}, u32[]{:S(2)}) copy-start(bf16[1,512,1024]{2,1,0:T(8,128)(2,1)} %param.19) | copy-start | bytes 3145732
  620.6 90.7 %copy-start.21 = (f32[1024]{0:T(1024)S(1)}, f32[1024]{0:T(1024)}, u32[]{:S(2)}) copy-start(f32[1024]{0:T(1024)} %param.21) | copy-start | bytes 12292
  620.6 90.7 %copy-start.25 = (f32[512]{0:T(512)S(1)}, f32[512]{0:T(512)}, u32[]{:S(2)}) copy-start(f32[512]{0:T(512)} %copy-done.24) | copy-start | bytes 6148
  620.6 290.1 %reduce-scatter.13.cloned.1.call-start = ((), (), s32[]{:S(2)}) async-start(), calls=%async_computation.12 | async-start | bytes 1179648 | tf_op jit(solution)/shard_map/reduce_scatter | solution.py:223
  625.5 129.4 %copy-start.37 = (f32[512]{0:T(512)S(1)}, f32[512]{0:T(512)}, u32[]{:S(2)}) copy-start(f32[512]{0:T(512)} %copy-done.36) | copy-start | bytes 6148
  (43 other events, 321.8 us)
Sparse Core Ops, SparseCore 0:
  11.6 37.1 all-gather.5
  51.5 50.0 all-gather.7
  103.1 32.9 all-gather.11
  138.1 40.3 all-gather.9
  260.2 67.2 reduce-scatter.16
  550.5 86.4 reduce-scatter.10
  639.8 71.4 reduce-scatter.8
  713.9 72.3 reduce-scatter.6
  790.3 53.4 reduce-scatter.14
  848.1 62.5 reduce-scatter.12
where the time goes:
time: 925 us; the launch traced here: 918 us
  waiting for transfers between devices  249 us (27%)
  matrix products  235 us (25%)
  blocking collectives  154 us (17%)
  other arithmetic  140 us (15%)
  local copies, waits for them, and re-layouts  123 us (13%)
  between operations  15.3 us (2%)
    dot_general x24, matrix products, step_block(): jnp.einsum('ijh,jhp->ihp', weights, x_block, precision=FULL_PRECISION)  78.3 us
    reduce_scatter x1, waiting for transfers between devices, body(): lax.psum_scatter(from_zx + lax.dot_general(grad_dt_low, dt_full, CONTRACT...  72 us
    reduce_scatter x1, waiting for transfers between devices, body(): lax.psum_scatter(grad_bc_w, 'dp', scatter_dimension=0, tiled=True)  66.8 us
    reduce_scatter x1, waiting for transfers between devices, body(): lax.psum_scatter(grad_dt_w, 'dp', scatter_dimension=0, tiled=True)  53.3 us
    psum x1, blocking collectives, body(): lax.psum((grad_norm_gain, widen(grad_x_taps, chan_start, total_channels),...  40.9 us
    psum x1, blocking collectives, body(): grad_bc_in = lax.psum(grad_bc_part, 'tensor').astype(jnp.bfloat16)  40.8 us
    another operation x73, other arithmetic  39.1 us
    dot_general x32, matrix products, step_block(): jnp.einsum('in,hpn->ihp', c_block, state, precision=FULL_PRECISION)  35.8 us
  transfers between devices with their start and end apart: 10, of which 6 were waited for; matrix products, arithmetic and copies ran while one was open for 53% of the time, Pallas kernels for 0%

commit v1 on v0

v1 whole, which is shorter than its diff:
```python
import functools

import jax
import jax.numpy as jnp
from jax import lax
from jax.experimental import pallas as pl
from jax.experimental.pallas import tpu as pltpu
from jax.sharding import PartitionSpec as P

BLOCK_LEN = 256
EPSILON = 1e-05
LANES = 128
HALO = 8
FAR = -1e30
F32 = jnp.float32
BF16 = jnp.bfloat16
CONTRACT_LAST = (((1,), (1,)), ((), ()))
CONTRACT_FIRST = (((0,), (0,)), ((), ()))


def mm(a, b):
    return jnp.dot(a, b, preferred_element_type=F32)


def mm_nt(a, b):
    return lax.dot_general(a, b, CONTRACT_LAST, preferred_element_type=F32)


def mm_tn(a, b):
    return lax.dot_general(a, b, CONTRACT_FIRST, preferred_element_type=F32)


def split_two(v):
    high = v.astype(BF16)
    return high, (v - high.astype(F32)).astype(BF16)


def split_three(v):
    first = v.astype(BF16)
    rest = v - first.astype(F32)
    second = rest.astype(BF16)
    return first, second, (rest - second.astype(F32)).astype(BF16)


def lanes_of(shape):
    return lax.broadcasted_iota(jnp.int32, shape, 1)


def rows_of(shape):
    return lax.broadcasted_iota(jnp.int32, shape, 0)


def spread_heads(v, spread, heads):
    first, second, third = split_three(v)
    lane = lanes_of(v.shape)
    packed = jnp.where(lane < heads, first.astype(F32), second.astype(F32))
    packed = jnp.where(lane < 2 * heads, packed, third.astype(F32))
    return mm(packed.astype(BF16), spread)


def head_sums(v, gather):
    high, low = split_two(v)
    return mm(high, gather) + mm(low, gather)


def tri_sums(tri, v):
    first, second, third = split_three(v)
    return mm(tri, first) + mm(tri, second) + mm(tri, third)


def spread_matrix(heads, channels):
    lane = rows_of((LANES, channels))
    head = lanes_of((LANES, channels)) // (channels // heads)
    return jnp.where((lane < 3 * heads) & (lane % heads == head), 1.0, 0.0).astype(BF16)


def gather_matrix(heads, channels):
    head = rows_of((channels, LANES)) // (channels // heads)
    return jnp.where(lanes_of((channels, LANES)) % heads == head, 1.0, 0.0).astype(BF16)


def conv_pre(buf, taps, length, tap_count):
    pre = taps[tap_count : tap_count + 1]
    for k in range(tap_count):
        pre = pre + taps[k : k + 1] * buf[pl.ds(HALO - tap_count + 1 + k, length), :]
    return pre


def fill(buf, prev_ref, cur_ref, is_first):
    prev = prev_ref[...]
    buf[0:HALO, :] = jnp.where(is_first, jnp.zeros_like(prev), prev)
    buf[HALO:, :] = cur_ref[...]


def step_values(dt_ref, ph):
    shifted = dt_ref[...] + ph[0:1]
    step_dt = jnp.maximum(shifted, 0.0) + jnp.log1p(jnp.exp(-jnp.abs(shifted)))
    log_step = step_dt * ph[1:2]
    return shifted, step_dt, log_step


def fwd_kernel(heads, gate_ref, xprev_ref, x_ref, bcprev_ref, bc_ref, dt_ref, gm_ref, px_ref, pbc_ref, ph_ref,
               mixed_ref, states_ref, sums_ref, xbuf, bcbuf, state, y_ref):
    step = pl.program_id(0)
    is_first = step == 0
    length, channels = x_ref.shape
    half = length // 2
    state_count = bc_ref.shape[1] // 2
    width = channels // heads

    @pl.when(is_first)
    def _():
        state[...] = jnp.zeros_like(state)

    fill(xbuf, xprev_ref, x_ref, is_first)
    fill(bcbuf, bcprev_ref, bc_ref, is_first)
    px, pbc, ph = px_ref[...], pbc_ref[...], ph_ref[...]
    x_low = jax.nn.silu(conv_pre(xbuf, px, length, 4)).astype(BF16)
    bc_low = jax.nn.silu(conv_pre(bcbuf, pbc, length, 4)).astype(BF16)
    b_low, c_low = bc_low[:, :state_count], bc_low[:, state_count:]
    _, step_dt, log_step = step_values(dt_ref, ph)
    tri = (rows_of((length, length)) >= lanes_of((length, length))).astype(F32).astype(BF16)
    cum = tri_sums(tri, log_step)
    cum_t = cum.T
    dt_t = step_dt.T
    spread = spread_matrix(heads, channels)
    exp_cum = spread_heads(jnp.exp(cum), spread, heads)
    weight = spread_heads(jnp.exp(cum[length - 1 : length] - cum) * step_dt, spread, heads)

    scores = mm_nt(c_low, b_low)
    lane = lanes_of((length, LANES))
    per_lane = LANES // width
    for group in range(heads // per_lane):
        cols = slice(group * LANES, (group + 1) * LANES)
        xp = x_low[:, cols]
        top = jnp.zeros((half, LANES), F32)
        bottom = jnp.zeros((half, LANES), F32)
        for s in range(per_lane):
            h = group * per_lane + s
            xm = jnp.where(lane // width == s, xp, jnp.zeros_like(xp))
            for part in range(2):
                r0, cn = part * half, (part + 1) * half
                rows = slice(r0, r0 + half)
                gaps = cum[rows, h : h + 1] - cum_t[h : h + 1, :cn]
                shape = (half, cn)
                keep = rows_of(shape) + r0 >= lanes_of(shape)
                decay = jnp.exp(jnp.where(keep, gaps, FAR))
                w = (scores[rows, :cn] * decay * dt_t[h : h + 1, :cn]).astype(BF16)
                if part == 0:
                    top = top + mm(w, xm[:cn])
                else:
                    bottom = bottom + mm(w, xm[:cn])
        y_ref[0:half, cols] = top
        y_ref[half:, cols] = bottom

    old = state[...]
    states_ref[0] = old
    old_high, old_low = split_two(old)
    carried = mm(c_low, old_high) + mm(c_low, old_low)
    x_wide = x_low.astype(F32)
    xw_high, xw_low = split_two(x_wide * weight)
    state[...] = old * exp_cum[length - 1 : length] + (mm_tn(b_low, xw_high) + mm_tn(b_low, xw_low))
    mixed = y_ref[...] + carried * exp_cum + px[6:7] * x_wide
    mixed_ref[...] = mixed
    gated = mixed * jax.nn.silu(gate_ref[...])
    squares = jnp.sum(gated * gated, axis=1, keepdims=True)
    inner = jnp.sum(gm_ref[...].astype(F32) * px[5:6] * gated, axis=1, keepdims=True)
    both = jnp.where(lane == 0, squares, jnp.where(lane == 1, inner, 0.0))
    sums_ref[0] = both.T[:8]


def bwd_kernel(heads, gate_ref, xprev_ref, x_ref, bcprev_ref, bc_ref, dt_ref, gm_ref, mixed_ref, states_ref, stats_ref,
               px_ref, pbc_ref, ph_ref, g_ref, gx_ref, gbc_ref, gh_ref, xbuf, bcbuf, gxbuf, gbcbuf, dstate, dx_ref, dg_ref):
    step = pl.program_id(0)
    is_first = step == pl.num_programs(0) - 1
    length, channels = x_ref.shape
    half = length // 2
    state_count = bc_ref.shape[1] // 2
    width = channels // heads

    @pl.when(step == 0)
    def _():
        dstate[...] = jnp.zeros_like(dstate)
        gxbuf[...] = jnp.zeros_like(gxbuf)
        gbcbuf[...] = jnp.zeros_like(gbcbuf)
        gx_ref[...] = jnp.zeros_like(gx_ref)
        gbc_ref[...] = jnp.zeros_like(gbc_ref)
        gh_ref[...] = jnp.zeros_like(gh_ref)

    fill(xbuf, xprev_ref, x_ref, is_first)
    fill(bcbuf, bcprev_ref, bc_ref, is_first)
    px, pbc, ph = px_ref[...], pbc_ref[...], ph_ref[...]
    pre_x = conv_pre(xbuf, px, length, 4)
    sig_x = jax.nn.sigmoid(pre_x)
    x_low = (pre_x * sig_x).astype(BF16)
    slope_x = sig_x * (1.0 + pre_x * (1.0 - sig_x))
    pre_bc = conv_pre(bcbuf, pbc, length, 4)
    sig_bc = jax.nn.sigmoid(pre_bc)
    bc_low = (pre_bc * sig_bc).astype(BF16)
    slope_bc = sig_bc * (1.0 + pre_bc * (1.0 - sig_bc))
    b_low, c_low = bc_low[:, :state_count], bc_low[:, state_count:]
    shifted, step_dt, log_step = step_values(dt_ref, ph)
    tri = (rows_of((length, length)) >= lanes_of((length, length))).astype(F32).astype(BF16)
    cum = tri_sums(tri, log_step)
    cum_t = cum.T
    spread = spread_matrix(heads, channels)
    gather = gather_matrix(heads, channels)
    exp_cum = spread_heads(jnp.exp(cum), spread, heads)
    weight = spread_heads(jnp.exp(cum[length - 1 : length] - cum) * step_dt, spread, heads)
    dt_wide = spread_heads(step_dt, spread, heads)
    x_wide = x_low.astype(F32)

    stats = stats_ref[0]
    stats = jnp.concatenate([stats, jnp.zeros((LANES - 8, length), F32)], axis=0).T
    rs, coef = stats[:, 0:1], stats[:, 1:2]
    gate = gate_ref[...]
    sig = jax.nn.sigmoid(gate)
    silu = gate * sig
    mixed = mixed_ref[...]
    gated = mixed * silu
    gm = gm_ref[...].astype(F32)
    ggated = rs * (gm * px[5:6]) - gated * coef
    d_gain = jnp.sum(gm * gated * rs, axis=0, keepdims=True)
    dy = ggated * silu
    g_ref[:, 0:channels] = (ggated * mixed * (sig * (1.0 + gate * (1.0 - sig)))).astype(BF16)
    dy_low = dy.astype(BF16)
    d_skip = jnp.sum(dy * x_wide, axis=0, keepdims=True)

    old = states_ref[0]
    old_high, old_low = split_two(old)
    ds = dstate[...]
    ds_high, ds_low = split_two(ds)
    dye = dy * exp_cum
    dye_low = dye.astype(BF16)
    dc = mm_nt(dye_low, old_high)
    carried = mm(c_low, old_high) + mm(c_low, old_low)
    from_carried = head_sums(dye * carried, gather)
    dxs = (mm(b_low, ds_high) + mm(b_low, ds_low)) * weight
    from_state = head_sums(x_wide * dxs, gather)
    db = mm_nt((x_wide * weight).astype(BF16), ds_high)
    last = exp_cum[length - 1 : length]
    decayed = jnp.sum(old * ds, axis=0, keepdims=True) * last
    decayed = head_sums(jnp.broadcast_to(decayed, (8, channels)), gather)[0:1]
    dstate[...] = ds * last + mm_tn(c_low, dye_low)

    scores = mm_nt(b_low, c_low)
    xdt_low = (x_wide * dt_wide).astype(BF16)
    lane = lanes_of((length, LANES))
    per_lane = LANES // width
    dg_ref[...] = jnp.zeros_like(dg_ref)
    col_sums = jnp.zeros((length, LANES), F32)
    row_sums = jnp.zeros((8, length), F32)
    row8 = rows_of((8, length))
    for group in range(heads // per_lane):
        cols = slice(group * LANES, (group + 1) * LANES)
        xp, dyp = xdt_low[:, cols], dy_low[:, cols]
        top = jnp.zeros((half, LANES), F32)
        bottom = jnp.zeros((half, LANES), F32)
        for s in range(per_lane):
            h = group * per_lane + s
            mine = lane // width == s
            xm = jnp.where(mine, xp, jnp.zeros_like(xp))
            dym = jnp.where(mine, dyp, jnp.zeros_like(dyp))
            col_parts = []
            row_parts = []
            for part in range(2):
                r0 = part * half
                rows = slice(r0, r0 + half)
                gaps = cum_t[h : h + 1, r0:] - cum[rows, h : h + 1]
                shape = (half, length - r0)
                keep = lanes_of(shape) >= rows_of(shape)
                decay = jnp.exp(jnp.where(keep, gaps, FAR))
                v = scores[rows, r0:] * decay
                dw = mm_nt(xm[rows], dyp[r0:])
                dg_ref[rows, r0:] += decay * dw
                e = v * dw
                col_parts.append(jnp.sum(e, axis=1, keepdims=True))
                row_parts.append(jnp.sum(e, axis=0, keepdims=True))
                if part == 0:
                    top = top + mm(v.astype(BF16), dym)
                else:
                    bottom = bottom + mm(v.astype(BF16), dym[r0:])
            col = jnp.concatenate(col_parts, axis=0)
            row = row_parts[0] + jnp.concatenate([jnp.zeros((1, half), F32), row_parts[1]], axis=1)
            col_sums = jnp.where(lane % heads == h, col, col_sums)
            row_sums = jnp.where(row8 == h, row, row_sums)
        dx_ref[0:half, cols] = top
        dx_ref[half:, cols] = bottom

    dg_low = dg_ref[...].astype(BF16)
    db = db + mm(dg_low, c_low)
    dc = dc + mm_tn(dg_low, b_low)
    dx = dx_ref[...] * dt_wide + dxs + px[6:7] * dy

    row_cols = jnp.concatenate([row_sums] * (LANES // 8), axis=0).T
    local = row_cols - col_sums + from_carried - from_state
    tri_up = (rows_of((length, length)) <= lanes_of((length, length))).astype(F32).astype(BF16)
    grad_log = tri_sums(tri_up, local) + (jnp.sum(from_state, axis=0, keepdims=True) + decayed)
    direct = jnp.where(step_dt > 0.0, (col_sums + from_state) / step_dt, 0.0)
    grad_dt = (direct + ph[1:2] * grad_log) * jax.nn.sigmoid(shifted)
    gh_ref[0:1] += jnp.sum(grad_dt, axis=0, keepdims=True)
    gh_ref[1:2] += jnp.sum(grad_log * log_step, axis=0, keepdims=True)
    g_ref[:, 2 * channels + 2 * state_count :] = jnp.where(lane < heads, grad_dt, 0.0).astype(BF16)

    def conv_back(grad, slope, buf, gbuf, taps, sums_ref):
        gbuf[length:, :] = gbuf[0:HALO, :]
        gp = grad * slope
        gbuf[0:length, :] = gp
        result = jnp.zeros_like(gp)
        for k in range(4):
            result = result + taps[k : k + 1] * gbuf[pl.ds(3 - k, length), :]
            sums_ref[k : k + 1] += jnp.sum(buf[pl.ds(HALO - 3 + k, length), :] * gp, axis=0, keepdims=True)
        sums_ref[4:5] += jnp.sum(gp, axis=0, keepdims=True)
        return result.astype(BF16)

    g_ref[:, channels : 2 * channels] = conv_back(dx, slope_x, xbuf, gxbuf, px, gx_ref)
    g_ref[:, 2 * channels : 2 * channels + 2 * state_count] = conv_back(
        jnp.concatenate([db, dc], axis=1), slope_bc, bcbuf, gbcbuf, pbc, gbc_ref
    )
    gx_ref[5:6] += d_gain
    gx_ref[6:7] += d_skip


def scan_specs(length, channels, states, block):
    halo = length // HALO

    def at(width, start):
        return pl.BlockSpec((length, width), lambda i: (block(i), start // width))

    def before(width, start):
        return pl.BlockSpec((HALO, width), lambda i: (jnp.maximum(block(i) * halo - 1, 0), start // width))

    return [
        at(channels, 0),
        before(channels, channels),
        at(channels, channels),
        before(2 * states, 2 * channels),
        at(2 * states, 2 * channels),
        at(LANES, 2 * channels + 2 * states),
    ]


def whole(shape):
    return pl.BlockSpec(shape, lambda i: (0,) * len(shape))


def mix_forward(proj, grad_mixed, px, pbc, ph, heads):
    tokens, channels = grad_mixed.shape
    states = pbc.shape[1] // 2
    length = BLOCK_LEN
    blocks = tokens // length
    block = lambda i: i
    return pl.pallas_call(
        functools.partial(fwd_kernel, heads),
        grid=(blocks,),
        in_specs=scan_specs(length, channels, states, block)
        + [pl.BlockSpec((length, channels), lambda i: (i, 0)), whole(px.shape), whole(pbc.shape), whole(ph.shape)],
        out_specs=[
            pl.BlockSpec((length, channels), lambda i: (i, 0)),
            pl.BlockSpec((1, states, channels), lambda i: (i, 0, 0)),
            pl.BlockSpec((1, 8, length), lambda i: (i, 0, 0)),
        ],
        out_shape=[
            jax.ShapeDtypeStruct((tokens, channels), F32),
            jax.ShapeDtypeStruct((blocks, states, channels), F32),
            jax.ShapeDtypeStruct((blocks, 8, length), F32),
        ],
        scratch_shapes=[
            pltpu.VMEM((length + HALO, channels), F32),
            pltpu.VMEM((length + HALO, 2 * states), F32),
            pltpu.VMEM((states, channels), F32),
            pltpu.VMEM((length, channels), F32),
        ],
        name="mix_forward",
    )(proj, proj, proj, proj, proj, proj, grad_mixed, px, pbc, ph)


def mix_backward(proj, grad_mixed, mixed, states_in, stats, px, pbc, ph, heads):
    tokens, channels = grad_mixed.shape
    states = pbc.shape[1] // 2
    length = BLOCK_LEN
    blocks = tokens // length
    block = lambda i: blocks - 1 - i
    total = 2 * channels + 2 * states + LANES
    return pl.pallas_call(
        functools.partial(bwd_kernel, heads),
        grid=(blocks,),
        in_specs=scan_specs(length, channels, states, block)
        + [
            pl.BlockSpec((length, channels), lambda i: (block(i), 0)),
            pl.BlockSpec((length, channels), lambda i: (block(i), 0)),
            pl.BlockSpec((1, states, channels), lambda i: (block(i), 0, 0)),
            pl.BlockSpec((1, 8, length), lambda i: (block(i), 0, 0)),
            whole(px.shape),
            whole(pbc.shape),
            whole(ph.shape),
        ],
        out_specs=[
            pl.BlockSpec((length, total), lambda i: (block(i), 0)),
            whole((8, channels)),
            whole((8, 2 * states)),
            whole((8, LANES)),
        ],
        out_shape=[
            jax.ShapeDtypeStruct((tokens, total), BF16),
            jax.ShapeDtypeStruct((8, channels), F32),
            jax.ShapeDtypeStruct((8, 2 * states), F32),
            jax.ShapeDtypeStruct((8, LANES), F32),
        ],
        scratch_shapes=[
            pltpu.VMEM((length + HALO, channels), F32),
            pltpu.VMEM((length + HALO, 2 * states), F32),
            pltpu.VMEM((length + HALO, channels), F32),
            pltpu.VMEM((length + HALO, 2 * states), F32),
            pltpu.VMEM((states, channels), F32),
            pltpu.VMEM((length, channels), F32),
            pltpu.VMEM((length, length), F32),
        ],
        name="mix_backward",
    )(proj, proj, proj, proj, proj, proj, grad_mixed, mixed, states_in, stats, px, pbc, ph)


def widen(piece, start, full_size):
    holder = jnp.zeros(piece.shape[:-1] + (full_size,), F32)
    return lax.dynamic_update_slice_in_dim(holder, piece, start, piece.ndim - 1)


def body(acts, grad_out, norm_gain, w_zx, w_bc, w_dt, w_out, conv_x, conv_x_bias, conv_bc, conv_bc_bias,
         dt_bias, a_log, d_skip, gate_gain):
    parts = lax.axis_size("tensor")
    rank = lax.axis_index("tensor")
    rows, features = acts.shape[1:]
    w_rows, _, channels = w_zx.shape
    heads = w_dt.shape[1]
    states = w_bc.shape[1] // 2
    width = channels // heads
    total_channels, total_heads = channels * parts, heads * parts
    chan_start, head_start = rank * channels, rank * heads
    repeat = LANES // heads
    side = 2 * channels + 2 * states + LANES

    local_w = jnp.concatenate([w_zx.reshape(w_rows, 2 * channels), w_bc, jnp.tile(w_dt, (1, repeat)), w_out], axis=1)
    w_all = lax.all_gather(local_w, "dp", axis=0, tiled=True)
    w_in, w_o = w_all[:, :side], w_all[:, side:]

    acts_row = acts[0].astype(F32)
    rs0 = lax.rsqrt(jnp.mean(acts_row * acts_row, axis=-1, keepdims=True) + EPSILON)
    hidden = lax.all_gather((acts_row * rs0 * norm_gain).astype(BF16), "tensor", axis=0, tiled=True)
    grad_rows = lax.all_gather(grad_out[0], "tensor", axis=0, tiled=True)
    proj = mm(hidden, w_in)
    grad_mixed = mm(grad_rows, w_o).astype(BF16)

    def take(v, start, size):
        return lax.dynamic_slice_in_dim(v, start, size, v.ndim - 1)

    gain = take(gate_gain, chan_start, channels)
    skip = jnp.repeat(take(d_skip, head_start, heads), width)
    px = jnp.concatenate(
        [take(conv_x, chan_start, channels), take(conv_x_bias, chan_start, channels)[None], gain[None], skip[None],
         jnp.zeros((1, channels), F32)], axis=0)
    pbc = jnp.concatenate([conv_bc, conv_bc_bias[None], jnp.zeros((3, 2 * states), F32)], axis=0)
    ph = jnp.stack([jnp.tile(take(dt_bias, head_start, heads), repeat),
                    jnp.tile(-jnp.exp(take(a_log, head_start, heads)), repeat)])
    ph = jnp.concatenate([ph, jnp.zeros((6, LANES), F32)], axis=0)

    mixed, state_in, sums = mix_forward(proj, grad_mixed, px, pbc, ph, heads)
    sums = lax.psum(sums[:, :2], "tensor")
    inv = lax.rsqrt(sums[:, 0] / total_channels + EPSILON)
    coef = inv * inv * inv * (sums[:, 1] / total_channels)
    stats = jnp.concatenate([jnp.stack([inv, coef], axis=1), jnp.zeros((inv.shape[0], 6, inv.shape[1]), F32)], axis=1)
    mixed_out = (mixed * jax.nn.silu(proj[:, :channels]) * inv.reshape(-1, 1) * gain).astype(BF16)
    projected = lax.psum_scatter(mm_nt(mixed_out, w_o).astype(BF16), "tensor", scatter_dimension=0, tiled=True)
    out_acts = (acts_row + projected.astype(F32)).astype(BF16)[None]
    grad_w_out = lax.psum_scatter(mm_tn(grad_rows, mixed_out).astype(BF16), "dp", scatter_dimension=0, tiled=True)

    g_all, gx, gbc, gh = mix_backward(proj, grad_mixed, mixed, state_in, stats, px, pbc, ph, heads)
    grad_hidden = lax.psum_scatter(mm_nt(g_all, w_in).astype(BF16), "tensor", scatter_dimension=0, tiled=True)
    grad_w = lax.psum_scatter(mm_tn(hidden, g_all).astype(BF16), "dp", scatter_dimension=0, tiled=True).astype(F32)
    grad_w_bc = lax.psum(grad_w[:, 2 * channels : 2 * channels + 2 * states], "tensor")

    grad_hidden = grad_hidden.astype(F32)
    grad_ng = jnp.sum(grad_hidden * acts_row * rs0, axis=0)
    pulled = grad_hidden * norm_gain
    inner = jnp.sum(pulled * acts_row, axis=-1, keepdims=True)
    grad_acts = grad_out[0].astype(F32) + pulled * rs0 - acts_row * (rs0 * rs0 * rs0 / features * inner)

    pieces = (
        grad_ng,
        widen(gx[0:4], chan_start, total_channels),
        widen(gx[4], chan_start, total_channels),
        gbc[0:4],
        gbc[4],
        widen(gh[0, :heads], head_start, total_heads),
        widen(gh[1, :heads], head_start, total_heads),
        widen(jnp.sum(gx[6].reshape(heads, width), axis=1), head_start, total_heads),
        widen(gx[5], chan_start, total_channels),
    )
    ng, cx, cxb, cbc, cbcb, dtb, alog, dsk, gg = lax.psum(pieces, ("dp", "tensor"))
    return (
        out_acts,
        grad_acts[None],
        ng,
        grad_w[:, : 2 * channels].reshape(w_rows, 2, channels),
        grad_w_bc,
        grad_w[:, 2 * channels + 2 * states : 2 * channels + 2 * states + heads],
        grad_w_out.astype(F32),
        cx,
        cxb,
        cbc,
        cbcb,
        dtb,
        alog,
        dsk,
        gg,
    )


def solution(mesh):
    in_specs = (
        P("dp", "tensor", None),
        P("dp", "tensor", None),
        P(),
        P("dp", None, "tensor"),
        P("dp", None),
        P("dp", "tensor"),
        P("dp", "tensor"),
    ) + (P(),) * 8
    out_specs = (
        P("dp", "tensor", None),
        P("dp", "tensor", None),
        P(),
        P("dp", None, "tensor"),
        P("dp", None),
        P("dp", "tensor"),
        P("dp", "tensor"),
    ) + (P(),) * 8
    return jax.shard_map(body, mesh=mesh, in_specs=in_specs, out_specs=out_specs, check_vma=False)
```

time: 925 us -> 495 us (0.54)
  matrix products: 235 us -> 49.7 us
  other arithmetic: 140 us -> 17.2 us
  local copies, waits for them, and re-layouts: 123 us -> 19.7 us
  blocking collectives: 154 us -> 50.9 us
  Pallas kernels: 0 us -> 73.8 us
  waiting for transfers between devices: 249 us -> 268 us
    dot_general x124 -> x6, matrix products: 235 us -> 49.7 us  [the longest x2 18 us: mm(): return jnp.dot(a, b, preferred_element_type=F32)]
    all_gather x4 -> x3, waiting for transfers between devices: 15.6 us -> 130 us  [the longest x1 72.9 us: body(): w_all = lax.all_gather(local_w, 'dp', axis=0, tiled=True)]
    reduce_scatter x6 -> x3, waiting for transfers between devices: 232 us -> 137 us  [the longest x1 51.2 us: body(): lax.psum_scatter(mm_tn(hidden, g_all).astype(BF16), 'dp', scatter_dimensi...]
    pallas_call x0 -> x2, Pallas kernels: none -> 73.8 us  [the longest x1 53.3 us: mix_backward(): pl.pallas_call(functools.partial(bwd_kernel, heads), grid=(blocks,), in_s...]
    all_gather x2 -> x0, blocking collectives: 60.1 us -> none  [the longest x1 32.3 us: body(): lax.all_gather(w_bc, 'dp', axis=0, tiled=True)]
    reshape x14 -> x1, local copies, waits for them, and re-layouts: 48.9 us -> 1.23 us  [body(): grad_w[:, :2 * channels].reshape(w_rows, 2, channels)]
    another operation x82 -> x0, other arithmetic: 46.4 us -> none
    psum x4 -> x2, blocking collectives: 94.3 us -> 50.9 us  [the longest x1 40.7 us: body(): lax.psum(pieces, ('dp', 'tensor'))]
  transfers between devices with their start and end apart: 10 -> 8, of which waited for: 6 -> 6; matrix products, arithmetic and copies ran while one was open for 53% -> 12% of each run, Pallas kernels for 0% -> 11%
where the time goes in v1:
time: 495 us; the launch traced here: 494 us
  waiting for transfers between devices  268 us (54%)
  Pallas kernels  73.8 us (15%)
  blocking collectives  50.9 us (10%)
  matrix products  49.7 us (10%)
  local copies, waits for them, and re-layouts  19.7 us (4%)
  other arithmetic  17.2 us (3%)
  between operations  14.4 us (3%)
    all_gather x1, waiting for transfers between devices, body(): w_all = lax.all_gather(local_w, 'dp', axis=0, tiled=True)  72.9 us
    pallas_call x1, Pallas kernels, mix_backward(): pl.pallas_call(functools.partial(bwd_kernel, heads), grid=(blocks,), in_s...  53.3 us
    reduce_scatter x1, waiting for transfers between devices, body(): lax.psum_scatter(mm_tn(hidden, g_all).astype(BF16), 'dp', scatter_dimensi...  51.2 us
    reduce_scatter x1, waiting for transfers between devices, body(): lax.psum_scatter(mm_nt(mixed_out, w_o).astype(BF16), 'tensor', scatter_di...  45 us
    reduce_scatter x1, waiting for transfers between devices, body(): lax.psum_scatter(mm_nt(g_all, w_in).astype(BF16), 'tensor', scatter_dimen...  41.1 us
    psum x1, blocking collectives, body(): lax.psum(pieces, ('dp', 'tensor'))  40.7 us
    all_gather x1, waiting for transfers between devices, body(): lax.all_gather((acts_row * rs0 * norm_gain).astype(BF16), 'tensor', axis=...  28.9 us
    all_gather x1, waiting for transfers between devices, body(): grad_rows = lax.all_gather(grad_out[0], 'tensor', axis=0, tiled=True)  28.1 us
  transfers between devices with their start and end apart: 8, of which 6 were waited for; matrix products, arithmetic and copies ran while one was open for 12% of the time, Pallas kernels for 11%

profile of v1, /device:TPU:0, one launch (start us, length us, event | category | flops | bytes accessed | tf_op | source)
XLA Modules:
  0.0 494.3 jit_solution(4435689210093322388)
XLA Ops:
  9.9 1.7 pad_maximum_fusion
  11.7 1.5 fusion.17
  18.8 28.1 %all-gather.9.cloned.1.call-done = bf16[1,2048,1024]{2,1,0:T(8,128)(2,1)} async-done(((bf16[1,512,1024]{2,1,0:T(8,128)(2,1)}), bf16[1,2048,1024]{2,1,0:T(8,128)(2,1)}) %all-gather.9.cloned.1.call-update) | async-done | bytes 4194320 | tf_op jit(solution)/shard_map/all_gather | solution.py:449
  46.9 72.9 %all-gather.7.cloned.1.call-done = bf16[1024,1920]{1,0:T(8,128)(2,1)} async-done(((bf16[128,1920]{1,0:T(8,128)(2,1)}), bf16[1024,1920]{1,0:T(8,128)(2,1)}) %all-gather.7.cloned.1.call-update) | async-done | bytes 3932176 | tf_op jit(solution)/shard_map/all_gather | solution.py:443
  119.8 6.1 %fusion.7.gm_ref = bf16[2048,512]{1,0:T(8,128)(2,1)} fusion(bf16[1,2048,1024]{2,1,0:T(8,128)(2,1)} %all-gather.9.cloned.1.call-done, bf16[1024,1920]{1,0:T(8,128)(2,1)} %all-gather.7.cloned.1.call-done), kind=kOutput, calls=%fused_computation.15 | convolution fusion | flops 2148532224 | bytes 7340032 | tf_op jit(solution)/shard_map/dot_general | solution.py:22
  125.9 28.9 %all-gather.5.cloned.1.call-done = bf16[2048,1024]{1,0:T(8,128)(2,1)} async-done(((bf16[512,1024]{1,0:T(8,128)(2,1)}), bf16[2048,1024]{1,0:T(8,128)(2,1)}) %all-gather.5.cloned.1.call-update) | async-done | bytes 4194320 | tf_op jit(solution)/shard_map/all_gather | solution.py:448
  154.8 11.8 %fusion.11.gate_ref.xprev_ref.x_ref.bcprev_ref.bc_ref.dt_ref = f32[2048,1408]{1,0:T(8,128)} fusion(bf16[2048,1024]{1,0:T(8,128)(2,1)} %all-gather.5.cloned.1.call-done, bf16[1024,1920]{1,0:T(8,128)(2,1)} %all-gather.7.cloned.1.call-done), kind=kOutput, calls=%fused_computation.18 | convolution fusion | flops 5905580032 | bytes 18612224 | tf_op jit(solution)/shard_map/dot_general | solution.py:22
  166.6 20.5 %mix_forward.1 = (f32[2048,512]{1,0:T(8,128)}, f32[8,128,512]{2,1,0:T(8,128)}, f32[8,8,256]{2,1,0:T(8,128)}) custom-call(f32[2048,1408]{1,0:T(8,128)} %fusion.11.gate_ref.xprev_ref.x_ref.bcprev_ref.bc_ref.dt_ref, f32[2048,1408]{1,0:T(8,128)} %fusion.11.gate_ref.xprev_ref.x_ref.bcprev_ref.bc_ref.dt_ref, ...), custom_call_target="tpu_custom_call" | custom-call | tf_op jit(solution)/shard_map/mix_forward/pallas_call | solution.py:353
  188.0 10.2 %psum.77 = f32[8,2,256]{2,1,0:T(2,128)S(1)} all-reduce(f32[8,2,256]{2,1,0:T(2,128)S(1)} %slice.54), channel_id=1, replica_groups=mesh['dp'=8,'tensor'=4] {'tensor'}, use_global_device_ids=true, to_apply=%region_1.0 | all-reduce | flops 4096 | bytes 32768 | tf_op jit(solution)/shard_map/psum | solution.py:467
  198.3 4.4 multiply_convert_fusion
  202.9 3.4 fusion.27
  206.3 2.3 copy.49
  209.5 53.3 %mix_backward.1 = (bf16[2048,1408]{1,0:T(8,128)(2,1)}, f32[8,512]{1,0:T(8,128)}, f32[8,256]{1,0:T(8,128)}, f32[8,128]{1,0:T(8,128)}) custom-call(f32[2048,1408]{1,0:T(8,128)} %fusion.11.gate_ref.xprev_ref.x_ref.bcprev_ref.bc_ref.dt_ref, f32[2048,1408]{1,0:T(8,128)} %fusion.11.gate_ref.xprev_ref.x_ref.bcprev_ref.bc_ref.dt_ref, ...), custom_call_target="tpu_custom_call" | custom-call | tf_op jit(solution)/shard_map/mix_backward/pallas_call | solution.py:385
  262.9 11.3 %convolution_convert_fusion = bf16[1024,1408]{1,0:T(8,128)(2,1)} fusion(bf16[2048,1024]{1,0:T(8,128)(2,1)} %all-gather.5.cloned.1.call-done, bf16[2048,1408]{1,0:T(8,128)(2,1)} %get-tuple-element.25), kind=kOutput, calls=%fused_computation.11 | convolution fusion | flops 5907021824 | bytes 12845056 | tf_op jit(solution)/shard_map/dot_general | solution.py:30
  274.3 11.5 %convolution_convert_fusion.1 = bf16[2048,1024]{1,0:T(8,128)(2,1)} fusion(bf16[2048,1408]{1,0:T(8,128)(2,1)} %get-tuple-element.25, bf16[1024,1920]{1,0:T(8,128)(2,1)} %all-gather.7.cloned.1.call-done), kind=kOutput, calls=%fused_computation.12 | convolution fusion | flops 5907677184 | bytes 12845056 | tf_op jit(solution)/shard_map/dot_general | solution.py:26
  286.0 5.6 %convolution_convert_fusion.2 = bf16[2048,1024]{1,0:T(8,128)(2,1)} fusion(bf16[2048,512]{1,0:T(8,128)(2,1)S(1)} %multiply_convert_fusion, bf16[1024,1920]{1,0:T(8,128)(2,1)} %all-gather.7.cloned.1.call-done), kind=kOutput, calls=%fused_computation.13 | convolution fusion | flops 2149580800 | bytes 7340032 | tf_op jit(solution)/shard_map/dot_general | solution.py:26
  296.7 51.2 %reduce-scatter.11.cloned.1.call-done = bf16[128,1408]{1,0:T(8,128)(2,1)} async-done(((bf16[1024,1408]{1,0:T(8,128)(2,1)}), bf16[128,1408]{1,0:T(8,128)(2,1)}) %reduce-scatter.11.cloned.1.call-update) | async-done | bytes 360464 | tf_op jit(solution)/shard_map/reduce_scatter | solution.py:478
  351.6 1.5 slice.74
  353.2 41.1 %reduce-scatter.9.cloned.1.call-done = bf16[512,1024]{1,0:T(8,128)(2,1)} async-done(((bf16[2048,1024]{1,0:T(8,128)(2,1)}), bf16[512,1024]{1,0:T(8,128)(2,1)}) %reduce-scatter.9.cloned.1.call-update) | async-done | bytes 1048592 | tf_op jit(solution)/shard_map/reduce_scatter | solution.py:477
  394.2 2.1 fusion.23
  396.4 45.0 %reduce-scatter.7.cloned.1.call-done = bf16[512,1024]{1,0:T(8,128)(2,1)} async-done(((bf16[2048,1024]{1,0:T(8,128)(2,1)}), bf16[512,1024]{1,0:T(8,128)(2,1)}) %reduce-scatter.7.cloned.1.call-update) | async-done | bytes 1048592 | tf_op jit(solution)/shard_map/reduce_scatter | solution.py:472
  441.3 4.0 fusion.16
  445.3 40.7 %all-reduce = (f32[1024]{0:T(1024)}, f32[4,2048]{1,0:T(4,128)}, f32[2048]{0:T(1024)}, f32[4,256]{1,0:T(4,128)}, f32[256]{0:T(256)}, /*index=5*/f32[32]{0:T(128)}, f32[32]{0:T(128)}, f32[32]{0:T(128)}, f32[2048]{0:T(1024)}) all-reduce(f32[1024]{0:T(1024)S(1)} %get-tuple-element.89, ...), channel_id=1, replica_groups=mesh['dp'=8,'tensor'=4] {'dp','tensor'}, use_global_device_ids=true, to_apply=%region_6.7 | all-reduce | flops 14688 | bytes 117504 | tf_op jit(solution)/shard_map/psum | solution.py:498
  485.9 1.6 copy.60
  (94 shorter events, 19.4 us)
Async XLA Ops:
  7.2 9.6 %copy-start = (f32[4,2048]{1,0:T(4,128)S(1)}, f32[4,2048]{1,0:T(4,128)}, u32[]{:S(2)}) copy-start(f32[4,2048]{1,0:T(4,128)} %param.22) | copy-start | bytes 98308
  7.2 6.0 %copy-start.1 = (bf16[1,512,1024]{2,1,0:T(8,128)(2,1)S(1)}, bf16[1,512,1024]{2,1,0:T(8,128)(2,1)}, u32[]{:S(2)}) copy-start(bf16[1,512,1024]{2,1,0:T(8,128)(2,1)} %param.15) | copy-start | bytes 3145732
  7.2 6.0 %copy-start.3 = (f32[1024]{0:T(1024)S(1)}, f32[1024]{0:T(1024)}, u32[]{:S(2)}) copy-start(f32[1024]{0:T(1024)} %param.17) | copy-start | bytes 12292
  7.2 7.3 %copy-start.9 = (f32[32]{0:T(128)S(1)}, f32[32]{0:T(128)}, u32[]{:S(2)}) copy-start(f32[32]{0:T(128)} %param.26) | copy-start | bytes 388
  7.2 7.4 %copy-start.10 = (f32[32]{0:T(128)S(1)}, f32[32]{0:T(128)}, u32[]{:S(2)}) copy-start(f32[32]{0:T(128)} %param.28) | copy-start | bytes 388
  7.2 9.3 %copy-start.11 = (f32[32]{0:T(128)S(1)}, f32[32]{0:T(128)}, u32[]{:S(2)}) copy-start(f32[32]{0:T(128)} %param.27) | copy-start | bytes 388
  7.3 10.9 %copy-start.7 = (f32[256]{0:T(256)S(1)}, f32[256]{0:T(256)}, u32[]{:S(2)}) copy-start(f32[256]{0:T(256)} %param.25) | copy-start | bytes 3076
  7.3 10.9 %copy-start.5 = (f32[4,256]{1,0:T(4,128)S(1)}, f32[4,256]{1,0:T(4,128)}, u32[]{:S(2)}) copy-start(f32[4,256]{1,0:T(4,128)} %param.24) | copy-start | bytes 12292
  7.3 39.6 %all-gather.9.cloned.1.call-start = ((), (), s32[]{:S(2)}) async-start(), calls=%async_computation.10 | async-start | bytes 5242880 | tf_op jit(solution)/shard_map/all_gather | solution.py:449
  8.0 111.8 %all-gather.7.cloned.1.call-start = ((), (), s32[]{:S(2)}) async-start(), calls=%async_computation.5 | async-start | bytes 4423680 | tf_op jit(solution)/shard_map/all_gather | solution.py:443
  11.6 143.2 %all-gather.5.cloned.1.call-start = ((), (), s32[]{:S(2)}) async-start(), calls=%async_computation.4 | async-start | bytes 5242880 | tf_op jit(solution)/shard_map/all_gather | solution.py:448
  14.5 280.4 %reduce-scatter.13.cloned.1.call-start = ((), (), s32[]{:S(2)}) async-start(), calls=%async_computation.11 | async-start | bytes 1179648
  198.3 4.7 copy-start.8
  208.6 139.4 %reduce-scatter.11.cloned.1.call-start = ((), (), s32[]{:S(2)}) async-start(), calls=%async_computation.8 | async-start | bytes 3244032 | tf_op jit(solution)/shard_map/reduce_scatter | solution.py:478
  274.2 120.0 %reduce-scatter.9.cloned.1.call-start = ((), (), s32[]{:S(2)}) async-start(), calls=%async_computation.7 | async-start | bytes 5242880 | tf_op jit(solution)/shard_map/reduce_scatter | solution.py:477
  285.8 155.6 %reduce-scatter.7.cloned.1.call-start = ((), (), s32[]{:S(2)}) async-start(), calls=%async_computation.6 | async-start | bytes 5242880 | tf_op jit(solution)/shard_map/reduce_scatter | solution.py:472
  291.6 0.7 copy-start.6
  291.6 0.7 copy-start.4
  291.6 149.7 %copy-start.2 = (bf16[1,512,1024]{2,1,0:T(8,128)(2,1)S(1)}, bf16[1,512,1024]{2,1,0:T(8,128)(2,1)}, u32[]{:S(2)}) copy-start(bf16[1,512,1024]{2,1,0:T(8,128)(2,1)} %param.16) | copy-start | bytes 3145732
  291.6 194.3 %all-reduce.3.cloned.1.call-start = ((), (), s32[]{:S(2)}) async-start(), calls=%async_computation.9 | async-start | bytes 262144 | tf_op jit(solution)/shard_map/psum | solution.py:479
Sparse Core Ops, SparseCore 0:
  9.7 37.1 all-gather.8
  49.6 70.0 all-gather.6
  121.9 32.8 all-gather.4
  208.7 64.5 reduce-scatter.12
  277.1 70.8 reduce-scatter.10
  350.5 43.6 reduce-scatter.8
  396.8 44.4 reduce-scatter.6
  444.3 31.4 all-reduce.2

commit v2 on v1

--- a/solution.py
+++ b/solution.py
@@ -420,6 +420,249 @@
     )(proj, proj, proj, proj, proj, proj, grad_mixed, mixed, states_in, stats, px, pbc, ph)
 
 
+MESH = pl.DeviceIdType.MESH
+PIECES = 4
+
+
+def remote(src, dst, send_sem, recv_sem, target):
+    return pltpu.make_async_remote_copy(
+        src_ref=src, dst_ref=dst, send_sem=send_sem, recv_sem=recv_sem, device_id=target, device_id_type=MESH
+    )
+
+
+def head_kernel(lines, hid_in, grad_in, win_in, wo_in, proj_out, gm_out, hid_out, hid_t_out, grad_out, win_out, wo_out,
+                hbuf, htbuf, gbuf, winbuf, wobuf, pbuf, mbuf, a_send, a_recv, w_send, w_recv, y_send, y_recv, l_sem, p_sem):
+    rank = lax.axis_index("tensor")
+    place = lax.axis_index("dp")
+    z, y = place // 2, place % 2
+    core, chip = rank % 2, rank // 2
+    partner = {"tensor": chip * 2 + (1 - core)}
+    across = {"tensor": (1 - chip) * 2 + core}
+    beside = {"dp": z * 2 + (1 - y)}
+    above = {"dp": place + 2}
+    below = {"dp": place - 2}
+    tokens = hid_in.shape[0]
+    piece = tokens // PIECES
+
+    barrier = pltpu.get_barrier_semaphore()
+    for target in (partner, across, beside):
+        pl.semaphore_signal(barrier, inc=1, device_id=target, device_id_type=MESH)
+
+    @pl.when(z < lines - 1)
+    def _():
+        pl.semaphore_signal(barrier, inc=1, device_id=above, device_id_type=MESH)
+
+    @pl.when(z > 0)
+    def _():
+        pl.semaphore_signal(barrier, inc=1, device_id=below, device_id_type=MESH)
+
+    weights = ((win_in, winbuf), (wo_in, wobuf))
+
+    def block_rows(owner, c):
+        return pl.ds(pl.multiple_of(owner * tokens + c * piece, piece), piece)
+
+    locals_ = []
+
+    def local(src, dst, k):
+        copy = pltpu.make_async_copy(src, dst, l_sem.at[k])
+        copy.start()
+        return copy
+
+    own_rows = pl.ds(pl.multiple_of(rank * tokens, tokens), tokens)
+    own_h = local(hid_in, hbuf.at[own_rows], 0)
+    own_g = local(grad_in, gbuf.at[own_rows], 1)
+    own_w = []
+    for w, (src, dst) in enumerate(weights):
+        rows = src.shape[0]
+        own_w.append(local(src, dst.at[pl.ds(pl.multiple_of(place * rows, rows), rows)], 2 + w))
+
+    neighbours = 3 + (z + lines - 1) // lines + (2 * lines - 2 - z) // lines
+    pl.semaphore_wait(barrier, neighbours)
+
+    def token_copy(a, kind, c):
+        src_in, buf = ((hid_in, hbuf), (grad_in, gbuf))[a]
+        if kind == 2:
+            owner = (1 - chip) * 2 + core
+            src = buf.at[block_rows(owner, c)]
+        else:
+            owner = rank
+            src = src_in.at[pl.ds(c * piece, piece)]
+        return remote(src, buf.at[block_rows(owner, c)], a_send.at[a, kind, c], a_recv.at[a, kind, c],
+                      across if kind == 1 else partner)
+
+    def shard(w, source, half):
+        src, dst = weights[w]
+        rows = src.shape[0] // 2
+        return dst.at[pl.ds(pl.multiple_of((source * 2 + y) * 2 * rows + half * rows, rows), rows)]
+
+    def shard_source(w, side, far, half):
+        if far == 0:
+            src, _ = weights[w]
+            rows = src.shape[0] // 2
+            return z, src.at[pl.ds(half * rows, rows)]
+        source = z - far if side == 0 else z + far
+        return source, shard(w, source, half)
+
+    def line_copy(w, side, far, half):
+        source, src = shard_source(w, side, far, half)
+        return remote(src, shard(w, source, half), w_send.at[w, side, far, half], w_recv.at[w, side, far + 1, half],
+                      above if side == 0 else below)
+
+    def beside_copy(w, side, far, half):
+        source, src = shard_source(w, side, far, half)
+        return remote(src, shard(w, source, half), y_send.at[w, side, far, half], y_recv.at[w, side, far, half], beside)
+
+    def has(side, far):
+        return z - far >= 0 if side == 0 else z + far <= lines - 1
+
+    def goes_on(side, far):
+        if side == 0:
+            return (z - far >= 0) & (z < lines - 1)
+        return (z + far <= lines - 1) & (z > 0)
+
+    def send_shard(w, far, half):
+        for side in range(2):
+            if far == 0:
+                pl.when(goes_on(side, 0))(lambda side=side: line_copy(w, side, 0, half).start())
+            else:
+                def arrive(side=side):
+                    line_copy(w, side, far - 1, half).wait_recv()
+                    pl.when(goes_on(side, far))(lambda: line_copy(w, side, far, half).start())
+                    beside_copy(w, side, far, half).start()
+                pl.when(has(side, far))(arrive)
+        if far == 0:
+            beside_copy(w, 0, 0, half).start()
+
+    for half in range(2):
+        send_shard(0, 0, half)
+    for c in range(PIECES):
+        token_copy(0, 1, c).start()
+    for c in range(PIECES):
+        token_copy(0, 0, c).start()
+
+    def pass_on(a, c):
+        token_copy(a, 1, c).wait_recv()
+        token_copy(a, 2, c).start()
+
+    events = []
+    for far in range(1, lines):
+        for half in range(2):
+            events.append(functools.partial(send_shard, 0, far, half))
+    for c in range(PIECES):
+        def step(c=c):
+            pass_on(0, c)
+            token_copy(1, 1, c).start()
+        events.insert(min(2 * c + 1, len(events)), step)
+    for event in events:
+        event()
+    for far in range(lines):
+        for half in range(2):
+            send_shard(1, far, half)
+    for c in range(PIECES):
+        token_copy(1, 0, c).start()
+
+    own_h.wait()
+    for c in range(PIECES):
+        token_copy(0, 0, c).wait_recv()
+        token_copy(0, 2, c).wait_recv()
+
+    def each_beside(w, act):
+        for far in range(lines):
+            for side in range(2):
+                if far == 0 and side == 1:
+                    continue
+                def go(side=side, far=far):
+                    for half in range(2):
+                        act(beside_copy(w, side, far, half))
+                pl.when(has(side, far))(go)
+
+    own_w[0].wait()
+    each_beside(0, lambda copy: copy.wait_recv())
+    outs = [local(hbuf, hid_out, 0), local(winbuf, win_out, 2)]
+
+    total = hbuf.shape[0]
+    block = pbuf.shape[1]
+    done = []
+    for b in range(total // block):
+        slot = b % 2
+        rows = pl.ds(b * block, block)
+        if b >= 2:
+            done[b - 2].wait()
+        pbuf[slot] = mm(hbuf[rows, :], winbuf[...])
+        copy = pltpu.make_async_copy(pbuf.at[slot], proj_out.at[rows], p_sem.at[slot])
+        copy.start()
+        done.append(copy)
+        htbuf[:, rows] = hbuf[rows, :].T
+        if b % 2 == 1 and b // 2 < PIECES:
+            pass_on(1, b // 2)
+    outs.append(local(htbuf, hid_t_out, 4))
+    own_g.wait()
+    own_w[1].wait()
+    each_beside(1, lambda copy: copy.wait_recv())
+    outs.append(local(wobuf, wo_out, 3))
+    for c in range(PIECES):
+        token_copy(1, 0, c).wait_recv()
+        token_copy(1, 2, c).wait_recv()
+    outs.append(local(gbuf, grad_out, 1))
+    for b in range(total // block):
+        rows = pl.ds(b * block, block)
+        mbuf[rows, :] = mm(gbuf[rows, :], wobuf[...]).astype(BF16)
+    outs.append(local(mbuf, gm_out, 5))
+
+    for copy in outs + done[-2:]:
+        copy.wait()
+    for a in range(2):
+        for kind in range(3):
+            for c in range(PIECES):
+                token_copy(a, kind, c).wait_send()
+    for w in range(2):
+        each_beside(w, lambda copy: copy.wait_send())
+        for far in range(lines - 1):
+            for side in range(2):
+                def go(side=side, far=far):
+                    for half in range(2):
+                        line_copy(w, side, far, half).wait_send()
+                pl.when(goes_on(side, far))(go)
+
+
+def gather_and_project(hidden, grads, w_in, w_o, lines):
+    parts = lax.axis_size("tensor")
+    tokens, features = hidden.shape
+    rows, side = w_in.shape
+    channels = w_o.shape[1]
+    total = tokens * parts
+    any_spec = pl.BlockSpec(memory_space=pl.ANY)
+    shapes = [
+        ((total, side), F32), ((total, channels), BF16), ((total, features), BF16), ((features, total), BF16),
+        ((total, features), BF16), ((2 * lines * rows, side), BF16), ((2 * lines * rows, channels), BF16),
+    ]
+    return pl.pallas_call(
+        functools.partial(head_kernel, lines),
+        in_specs=[any_spec] * 4,
+        out_specs=[any_spec] * len(shapes),
+        out_shape=[jax.ShapeDtypeStruct(*s) for s in shapes],
+        scratch_shapes=[
+            pltpu.VMEM((total, features), BF16),
+            pltpu.VMEM((features, total), BF16),
+            pltpu.VMEM((total, features), BF16),
+            pltpu.VMEM((2 * lines * rows, side), BF16),
+            pltpu.VMEM((2 * lines * rows, channels), BF16),
+            pltpu.VMEM((2, BLOCK_LEN, side), F32),
+            pltpu.VMEM((total, channels), BF16),
+            pltpu.SemaphoreType.DMA((2, 3, PIECES)),
+            pltpu.SemaphoreType.DMA((2, 3, PIECES)),
+            pltpu.SemaphoreType.DMA((2, 2, lines, 2)),
+            pltpu.SemaphoreType.DMA((2, 2, lines + 1, 2)),
+            pltpu.SemaphoreType.DMA((2, 2, lines, 2)),
+            pltpu.SemaphoreType.DMA((2, 2, lines, 2)),
+            pltpu.SemaphoreType.DMA((6,)),
+            pltpu.SemaphoreType.DMA((2,)),
+        ],
+        compiler_params=pltpu.CompilerParams(collective_id=0, has_side_effects=True),
+        name="gather_and_project",
+    )(hidden, grads, w_in, w_o)
+
+
 def widen(piece, start, full_size):
     holder = jnp.zeros(piece.shape[:-1] + (full_size,), F32)
     return lax.dynamic_update_slice_in_dim(holder, piece, start, piece.ndim - 1)
@@ -437,18 +680,13 @@
     total_channels, total_heads = channels * parts, heads * parts
     chan_start, head_start = rank * channels, rank * heads
     repeat = LANES // heads
-    side = 2 * channels + 2 * states + LANES
-
-    local_w = jnp.concatenate([w_zx.reshape(w_rows, 2 * channels), w_bc, jnp.tile(w_dt, (1, repeat)), w_out], axis=1)
-    w_all = lax.all_gather(local_w, "dp", axis=0, tiled=True)
-    w_in, w_o = w_all[:, :side], w_all[:, side:]
 
     acts_row = acts[0].astype(F32)
     rs0 = lax.rsqrt(jnp.mean(acts_row * acts_row, axis=-1, keepdims=True) + EPSILON)
-    hidden = lax.all_gather((acts_row * rs0 * norm_gain).astype(BF16), "tensor", axis=0, tiled=True)
-    grad_rows = lax.all_gather(grad_out[0], "tensor", axis=0, tiled=True)
-    proj = mm(hidden, w_in)
-    grad_mixed = mm(grad_rows, w_o).astype(BF16)
+    local_w = jnp.concatenate([w_zx.reshape(w_rows, 2 * channels), w_bc, jnp.tile(w_dt, (1, repeat))], axis=1)
+    proj, grad_mixed, hidden, hidden_t, grad_rows, w_in, w_o = gather_and_project(
+        (acts_row * rs0 * norm_gain).astype(BF16), grad_out[0], local_w, w_out, lax.axis_size("dp") // 2
+    )
 
     def take(v, start, size):
         return lax.dynamic_slice_in_dim(v, start, size, v.ndim - 1)

time: 495 us -> 403 us (0.81)
  waiting for transfers between devices: 268 us -> 137 us
  Pallas kernels: 73.8 us -> 131 us
  matrix products: 49.7 us -> 31.7 us
    all_gather x3 -> x0, waiting for transfers between devices: 130 us -> none  [the longest x1 72.9 us: body(): w_all = lax.all_gather(local_w, 'dp', axis=0, tiled=True)]
    pallas_call x0 -> x1, Pallas kernels: none -> 57.4 us  [gather_and_project(): pl.pallas_call(functools.partial(head_kernel, lines), in_specs=[any_spec]...]
    dot_general x2 -> x0, matrix products: 18 us -> none  [mm(): return jnp.dot(a, b, preferred_element_type=F32)]
  transfers between devices with their start and end apart: 8 -> 5, of which waited for: 6 -> 3; matrix products, arithmetic and copies ran while one was open for 12% -> 11% of each run, Pallas kernels for 11% -> 13%
where the time goes in v2:
time: 403 us; the launch traced here: 402 us
  waiting for transfers between devices  137 us (34%)
  Pallas kernels  131 us (33%)
  blocking collectives  51.1 us (13%)
  matrix products  31.7 us (8%)
  other arithmetic  19.8 us (5%)
  local copies, waits for them, and re-layouts  16.8 us (4%)
  between operations  14 us (3%)
    pallas_call x1, Pallas kernels, gather_and_project(): pl.pallas_call(functools.partial(head_kernel, lines), in_specs=[any_spec]...  57.4 us
    pallas_call x1, Pallas kernels, mix_backward(): pl.pallas_call(functools.partial(bwd_kernel, heads), grid=(blocks,), in_s...  53.3 us
    reduce_scatter x1, waiting for transfers between devices, body(): lax.psum_scatter(mm_tn(hidden, g_all).astype(BF16), 'dp', scatter_dimensi...  50.7 us
    reduce_scatter x1, waiting for transfers between devices, body(): lax.psum_scatter(mm_nt(mixed_out, w_o).astype(BF16), 'tensor', scatter_di...  44.8 us
    reduce_scatter x1, waiting for transfers between devices, body(): lax.psum_scatter(mm_nt(g_all, w_in).astype(BF16), 'tensor', scatter_dimen...  41.2 us
    psum x1, blocking collectives, body(): lax.psum(pieces, ('dp', 'tensor'))  40.6 us
    pallas_call x1, Pallas kernels, mix_forward(): pl.pallas_call(functools.partial(fwd_kernel, heads), grid=(blocks,), in_s...  20.5 us
    dot_general x2, matrix products, mm_nt(): return lax.dot_general(a, b, CONTRACT_LAST, preferred_element_type=F32)  17 us
  transfers between devices with their start and end apart: 5, of which 3 were waited for; matrix products, arithmetic and copies ran while one was open for 11% of the time, Pallas kernels for 13%

profile of v2, /device:TPU:0, one launch (start us, length us, event | category | flops | bytes accessed | tf_op | source)
XLA Modules:
  0.0 401.9 jit_solution(12295470786772990220)
XLA Ops:
  11.3 1.5 fusion.4
  12.9 1.0 copy.38
  14.8 2.5 fusion.6.hid_in
  19.4 57.4 %gather_and_project.1 = (f32[2048,1408]{1,0:T(8,128)}, bf16[2048,512]{1,0:T(8,128)(2,1)}, bf16[2048,1024]{1,0:T(8,128)(2,1)}, bf16[1024,2048]{1,0:T(8,128)(2,1)}...) custom-call(bf16[512,1024]{1,0:T(8,128)(2,1)} %fusion.6.hid_in, ...), custom_call_target="tpu_custom_call" | custom-call | tf_op jit(solution)/shard_map/gather_and_project/pallas_call | solution.py:639
  77.5 20.5 %mix_forward.1 = (f32[2048,512]{1,0:T(8,128)}, f32[8,128,512]{2,1,0:T(8,128)}, f32[8,8,256]{2,1,0:T(8,128)}) custom-call(f32[2048,1408]{1,0:T(8,128)} %get-tuple-element.28.gate_ref.xprev_ref.x_ref.bcprev_ref.bc_ref.dt_ref, f32[2048,1408]{1,0:T(8,128)} %get-tuple-element.28.gate_ref.xprev_ref.x_ref.bcprev_ref.bc_ref.dt_ref, ...), custom_call_target="tpu_custom_call" | custom-call | tf_op jit(solution)/shard_map/mix_forward/pallas_call | solution.py:353
  98.0 0.8 slice.46
  98.8 10.5 %psum.77 = f32[8,2,256]{2,1,0:T(2,128)S(1)} all-reduce(f32[8,2,256]{2,1,0:T(2,128)S(1)} %slice.46), channel_id=1, replica_groups=mesh['dp'=8,'tensor'=4] {'tensor'}, use_global_device_ids=true, to_apply=%region_1.0 | all-reduce | flops 4096 | bytes 32768 | tf_op jit(solution)/shard_map/psum | solution.py:705
  109.4 4.4 %multiply_convert_fusion = bf16[2048,512]{1,0:T(8,128)(2,1)S(1)} fusion(f32[2048,512]{1,0:T(8,128)} %get-tuple-element.30.mixed_ref, f32[2048,1408]{1,0:T(8,128)} %get-tuple-element.28.gate_ref.xprev_ref.x_ref.bcprev_ref.bc_ref.dt_ref, f32[512]{0:T(512)S(1)} %dynamic_slice.20, f32[2048]{0:T(1024)S(1)} %bitcast.40), kind=kLoop, calls=%fused_computation.6 | loop fusion | flops 8388608 | bytes 10496000 | tf_op jit(solution)/shard_map/convert_element_type | solution.py:709
  114.0 3.4 convolution_convert_fusion.3
  118.2 53.3 %mix_backward.1 = (bf16[2048,1408]{1,0:T(8,128)(2,1)}, f32[8,512]{1,0:T(8,128)}, f32[8,256]{1,0:T(8,128)}, f32[8,128]{1,0:T(8,128)}) custom-call(f32[2048,1408]{1,0:T(8,128)} %get-tuple-element.28.gate_ref.xprev_ref.x_ref.bcprev_ref.bc_ref.dt_ref, f32[2048,1408]{1,0:T(8,128)} %get-tuple-element.28.gate_ref.xprev_ref.x_ref.bcprev_ref.bc_ref.dt_ref, ...), custom_call_target="tpu_custom_call" | custom-call | tf_op jit(solution)/shard_map/mix_backward/pallas_call | solution.py:385
  171.5 11.3 %convolution_convert_fusion = bf16[1024,1408]{1,0:T(8,128)(2,1)} fusion(bf16[2048,1024]{1,0:T(8,128)(2,1)} %get-tuple-element.36, bf16[2048,1408]{1,0:T(8,128)(2,1)} %get-tuple-element.34), kind=kOutput, calls=%fused_computation.7 | convolution fusion | flops 5907021824 | bytes 12845056 | tf_op jit(solution)/shard_map/dot_general | solution.py:30
  183.1 11.5 %convolution_convert_fusion.1 = bf16[2048,1024]{1,0:T(8,128)(2,1)} fusion(bf16[2048,1408]{1,0:T(8,128)(2,1)} %get-tuple-element.34, bf16[1024,1408]{1,0:T(8,128)(2,1)} %get-tuple-element.35), kind=kOutput, calls=%fused_computation.8 | convolution fusion | flops 5907677184 | bytes 12845056 | tf_op jit(solution)/shard_map/dot_general | solution.py:26
  194.7 5.6 %convolution_convert_fusion.2 = bf16[2048,1024]{1,0:T(8,128)(2,1)} fusion(bf16[2048,512]{1,0:T(8,128)(2,1)S(1)} %multiply_convert_fusion, bf16[1024,512]{1,0:T(8,128)(2,1)} %get-tuple-element.32), kind=kOutput, calls=%fused_computation.9 | convolution fusion | flops 2149580800 | bytes 7340032 | tf_op jit(solution)/shard_map/dot_general | solution.py:26
  203.5 1.6 convert_element_type.55
  205.2 50.7 %reduce-scatter.9.cloned.1.call-done = bf16[128,1408]{1,0:T(8,128)(2,1)} async-done(((bf16[1024,1408]{1,0:T(8,128)(2,1)}), bf16[128,1408]{1,0:T(8,128)(2,1)}) %reduce-scatter.9.cloned.1.call-update) | async-done | bytes 360464 | tf_op jit(solution)/shard_map/reduce_scatter | solution.py:716
  255.8 1.0 slice.62
  256.8 1.2 reshape.80
  259.5 1.5 slice.63
  261.0 41.2 %reduce-scatter.7.cloned.1.call-done = bf16[512,1024]{1,0:T(8,128)(2,1)} async-done(((bf16[2048,1024]{1,0:T(8,128)(2,1)}), bf16[512,1024]{1,0:T(8,128)(2,1)}) %reduce-scatter.7.cloned.1.call-update) | async-done | bytes 1048592 | tf_op jit(solution)/shard_map/reduce_scatter | solution.py:715
  302.2 2.1 fusion.10
  304.3 44.8 %reduce-scatter.5.cloned.1.call-done = bf16[512,1024]{1,0:T(8,128)(2,1)} async-done(((bf16[2048,1024]{1,0:T(8,128)(2,1)}), bf16[512,1024]{1,0:T(8,128)(2,1)}) %reduce-scatter.5.cloned.1.call-update) | async-done | bytes 1048592 | tf_op jit(solution)/shard_map/reduce_scatter | solution.py:710
  349.2 4.0 fusion.3
  353.1 40.6 %all-reduce = (f32[1024]{0:T(1024)}, f32[4,2048]{1,0:T(4,128)}, f32[2048]{0:T(1024)}, f32[4,256]{1,0:T(4,128)}, f32[256]{0:T(256)}, /*index=5*/f32[32]{0:T(128)}, f32[32]{0:T(128)}, f32[32]{0:T(128)}, f32[2048]{0:T(1024)}) all-reduce(f32[1024]{0:T(1024)S(1)} %get-tuple-element.86, ...), channel_id=1, replica_groups=mesh['dp'=8,'tensor'=4] {'dp','tensor'}, use_global_device_ids=true, to_apply=%region_6.7 | all-reduce | flops 14688 | bytes 117504 | tf_op jit(solution)/shard_map/psum | solution.py:736
  393.8 1.6 copy.47
  (80 shorter events, 13.9 us)
Async XLA Ops:
  7.2 0.9 copy-start
  7.2 10.8 %copy-start.4 = (bf16[128,256]{1,0:T(8,128)(2,1)S(1)}, bf16[128,256]{1,0:T(8,128)(2,1)}, u32[]{:S(2)}) copy-start(bf16[128,256]{1,0:T(8,128)(2,1)} %param.19) | copy-start | bytes 196612
  7.2 11.6 %copy-start.9 = (f32[256]{0:T(256)S(1)}, f32[256]{0:T(256)}, u32[]{:S(2)}) copy-start(f32[256]{0:T(256)} %param.25) | copy-start | bytes 3076
  7.2 11.5 %copy-start.7 = (f32[4,256]{1,0:T(4,128)S(1)}, f32[4,256]{1,0:T(4,128)}, u32[]{:S(2)}) copy-start(f32[4,256]{1,0:T(4,128)} %param.24) | copy-start | bytes 12292
  7.2 196.3 %reduce-scatter.11.cloned.1.call-start = ((), (), s32[]{:S(2)}) async-start(), calls=%async_computation.8 | async-start | bytes 1179648 | tf_op jit(solution)/shard_map/reduce_scatter | solution.py:712
  109.3 4.7 %copy-start.10 = (bf16[2048,1024]{1,0:T(8,128)(2,1)S(1)}, bf16[2048,1024]{1,0:T(8,128)(2,1)}, u32[]{:S(2)}) copy-start(bf16[2048,1024]{1,0:T(8,128)(2,1)} %get-tuple-element.37) | copy-start | bytes 12582916
  117.4 138.4 %reduce-scatter.9.cloned.1.call-start = ((), (), s32[]{:S(2)}) async-start(), calls=%async_computation.6 | async-start | bytes 3244032 | tf_op jit(solution)/shard_map/reduce_scatter | solution.py:716
  182.9 119.4 %reduce-scatter.7.cloned.1.call-start = ((), (), s32[]{:S(2)}) async-start(), calls=%async_computation.5 | async-start | bytes 5242880 | tf_op jit(solution)/shard_map/reduce_scatter | solution.py:715
  194.6 154.5 %reduce-scatter.5.cloned.1.call-start = ((), (), s32[]{:S(2)}) async-start(), calls=%async_computation.4 | async-start | bytes 5242880 | tf_op jit(solution)/shard_map/reduce_scatter | solution.py:710
  200.2 0.7 copy-start.8
  200.2 0.7 copy-start.6
  200.2 102.0 %copy-start.2 = (bf16[1,512,1024]{2,1,0:T(8,128)(2,1)S(1)}, bf16[1,512,1024]{2,1,0:T(8,128)(2,1)}, u32[]{:S(2)}) copy-start(bf16[1,512,1024]{2,1,0:T(8,128)(2,1)} %param.15) | copy-start | bytes 3145732
  200.3 102.0 %copy-start.5 = (f32[1024]{0:T(1024)S(1)}, f32[1024]{0:T(1024)}, u32[]{:S(2)}) copy-start(f32[1024]{0:T(1024)} %param.17) | copy-start | bytes 12292
  200.3 148.9 %copy-start.3 = (bf16[1,512,1024]{2,1,0:T(8,128)(2,1)S(1)}, bf16[1,512,1024]{2,1,0:T(8,128)(2,1)}, u32[]{:S(2)}) copy-start(bf16[1,512,1024]{2,1,0:T(8,128)(2,1)} %param.16) | copy-start | bytes 3145732
  200.3 193.5 %all-reduce.3.cloned.1.call-start = ((), (), s32[]{:S(2)}) async-start(), calls=%async_computation.7 | async-start | bytes 262144 | tf_op jit(solution)/shard_map/psum | solution.py:717
  304.3 91.0 %copy-start.1 = (f32[4,2048]{1,0:T(4,128)S(1)}, f32[4,2048]{1,0:T(4,128)}, u32[]{:S(2)}) copy-start(f32[4,2048]{1,0:T(4,128)} %param.22) | copy-start | bytes 98308
Sparse Core Ops, SparseCore 0:
  117.5 63.4 reduce-scatter.10
  185.0 70.7 reduce-scatter.8
  258.5 43.6 reduce-scatter.6
  304.6 44.5 reduce-scatter.4
  352.0 31.4 all-reduce.2
